TPU v7x, 32 devices: a whole 2x2x4 slice. The times are simulated.
32 devices in a mesh: patch: 32 (over z, y, x, core).
Axes of the slice: x: 2, y: 2, z: 4, core: 2. Of those that a mesh axis runs over, the one named last changes fastest.
Arguments:
- atm_flux: bfloat16 [8, 98304], P(None, 'patch'), may hold values from -6 to 6
- remap_send: int32 [32, 5, 8], P('patch'), may hold values from 0 to 23
- remap_target: int32 [32, 5, 8], P('patch'), may hold values from 0 to 31
- remap_counts: int32 [32, 5], P('patch'), may hold values from 0 to 8, as said below
- remap_weights: bfloat16 [32, 5, 8, 128, 128], P('patch'), may hold values from -0.5 to 0.5
- coupling: float32 [2, 8], replicated, may hold values from -2 to 2
- tracer: float32 [2, 128, 131072], P(None, None, 'patch'), may hold values from -6 to 6
- wet: int32 [131072], P('patch'), may hold values from 0 to 1
- mix_inverse: float32 [1024, 128, 128], P('patch')
- halo_send: int32 [32, 4, 2, 128], P('patch'), may hold values from 0 to 4095
- halo_ghost: int32 [32, 4, 2, 128], P('patch'), may hold values from 0 to 4095
- halo_rows: int32 [32, 4], P('patch'), may hold values from 0 to 2, as said below
Outputs:
- ocean_flux: float32 [8, 131072], P(None, 'patch')
- tracer_out: float32 [2, 128, 131072], P(None, None, 'patch')
Inputs may be any that keep to these rules, and one draw needn't show every extreme that they name: `remap_counts`: some entry equals 8. `halo_rows`: some entry equals 2.
All inputs are finite; a program needn't handle non-finite values.
Results may differ from a plain program's by a relative error of at most 0.0003.
Values may be sent and summed in bfloat16 or wider, within the bound.
A program may use at most 64 MiB of HBM per device.

v0:
```python
import jax
import jax.numpy as jnp
from jax import lax
from jax.experimental import pallas as pl
from jax.experimental.pallas import tpu as pltpu
from jax.sharding import PartitionSpec as P

MESH = pl.DeviceIdType.MESH
CHUNKS = 8
TILE = 512


def split(value):
    high = value.astype(jnp.bfloat16)
    return high, (value - high.astype(jnp.float32)).astype(jnp.bfloat16)


def product(left, right):
    return jnp.dot(left, right, preferred_element_type=jnp.float32)


def couple_kernel(
    remap_send,
    remap_target,
    remap_counts,
    coupling,
    halo_rows,
    atm,
    wet,
    halo_send,
    halo_ghost,
    weights_hbm,
    tracer_hbm,
    inverse_hbm,
    flux_out,
    mixed,
    received,
    scatter,
    weights,
    tracer,
    inverse,
    sent,
    surface,
    total,
    outgoing,
    arrived,
    tables,
    picked,
    load_sem,
    flux_send_sem,
    flux_recv_sem,
    halo_send_sem,
    halo_recv_sem,
):
    size = lax.axis_size("patch")
    me = lax.axis_index("patch")
    spans, slots = remap_send.shape[0], remap_send.shape[2]
    radius = spans // 2
    tracers, levels, cells = tracer.shape
    block = weights.shape[-1]
    blocks = cells // block
    fluxes = atm.shape[0]
    steps = [d - radius for d in range(spans) if d != radius]
    depth, lanes = halo_send.shape[2], halo_send.shape[3]

    def peer(step):
        return lax.rem(me + step + size, size)

    weight_load = pltpu.make_async_copy(weights_hbm.at[0], weights, load_sem.at[2 * CHUNKS])
    weight_load.start()
    part, span = blocks // CHUNKS, cells // CHUNKS
    loads = []
    for chunk in range(CHUNKS):
        run = pl.ds(chunk * span, span)
        loads.append(
            pltpu.make_async_copy(
                tracer_hbm.at[:, :, run], tracer.at[:, :, run], load_sem.at[2 * chunk]
            )
        )
        group = pl.ds(chunk * part, part)
        loads.append(
            pltpu.make_async_copy(
                inverse_hbm.at[group], inverse.at[group], load_sem.at[2 * chunk + 1]
            )
        )
    for load in loads:
        load.start()

    barrier = pltpu.get_barrier_semaphore()
    for step in steps:
        pl.semaphore_signal(barrier, inc=1, device_id=(peer(step),), device_id_type=MESH)
    sources = [
        atm[:, a * block : (a + 1) * block].astype(jnp.float32)
        for a in range(atm.shape[1] // block)
    ]
    blank = jnp.zeros((fluxes, block), jnp.int32)
    for d in range(spans):
        for c in range(slots):
            wanted = blank + remap_send[d, 0, c]
            piece = sources[0]
            for a in range(1, len(sources)):
                piece = jnp.where(wanted == a, sources[a], piece)
            piece = piece.astype(jnp.bfloat16)
            if d == radius:
                arrived[d, c] = piece
            else:
                outgoing[d, c] = piece
    pl.semaphore_wait(barrier, len(steps))
    flux_copies = []
    for d in range(spans):
        if d == radius:
            continue
        copy = pltpu.make_async_remote_copy(
            src_ref=outgoing.at[d],
            dst_ref=arrived.at[d],
            send_sem=flux_send_sem.at[d],
            recv_sem=flux_recv_sem.at[d],
            device_id=(peer(d - radius),),
            device_id_type=MESH,
        )
        copy.start()
        flux_copies.append(copy)

    rows = 512

    def table_rows(index, _):
        base = pl.multiple_of(index * rows, rows)
        ids = lax.broadcasted_iota(jnp.int32, (rows, lanes), 0) + base
        for h in range(len(steps)):
            for r in range(depth):
                hit = ids == halo_send[0, h, r : r + 1, :]
                tables[h, pl.ds(base, rows), r * lanes : (r + 1) * lanes] = jnp.where(
                    hit, 1.0, 0.0
                ).astype(jnp.bfloat16)
        return 0

    lax.fori_loop(0, cells // rows, table_rows, 0)

    weight_load.wait()
    for copy in flux_copies:
        copy.wait()
    owner = lax.broadcasted_iota(jnp.int32, (blocks, fluxes, block), 0)
    for d in range(spans):
        pieces = []
        for c in range(slots):
            used = (blank + remap_counts[0, d]) > c
            piece = jnp.where(used, arrived[d, c].astype(jnp.float32), 0.0)
            placed = jnp.where(owner == remap_target[d, 0, c], piece[None], 0.0)
            pieces.append(placed.reshape(blocks * fluxes, block).astype(jnp.bfloat16))
        left = jnp.concatenate(pieces, axis=1)
        term = product(left, weights[d].reshape(slots * block, block))
        if d == 0:
            total[...] = term
        else:
            total[...] += term
    for b in range(blocks):
        run = slice(b * block, (b + 1) * block)
        flux = total[b * fluxes : (b + 1) * fluxes, :] * wet[0:1, run].astype(jnp.float32)
        flux_out[:, run] = flux
        for t in range(tracers):
            value = coupling[t, 0] * flux[0:1, :]
            for f in range(1, fluxes):
                value = value + coupling[t, f] * flux[f : f + 1, :]
            surface[t : t + 1, run] = value

    top = lax.broadcasted_iota(jnp.int32, (levels, block), 0) == 0

    def mix_block(k):
        run = slice(k * block, (k + 1) * block)
        high, low = split(inverse[k])
        wetf = wet[0:1, run].astype(jnp.float32)
        held = [tracer[t, :, run] for t in range(tracers)]
        right = jnp.concatenate(
            [
                held[t] + jnp.where(top, surface[t : t + 1, run], 0.0)
                for t in range(tracers)
            ],
            axis=1,
        )
        right_high, right_low = split(right)
        solved = (
            product(high, right_high) + product(high, right_low) + product(low, right_high)
        )
        for t in range(tracers):
            value = wetf * solved[:, t * block : (t + 1) * block] + (1.0 - wetf) * held[t]
            mixed[t, :, run] = value
            sent[t * levels : (t + 1) * levels, run] = value.astype(jnp.bfloat16)

    for chunk in range(CHUNKS):
        loads[2 * chunk].wait()
        loads[2 * chunk + 1].wait()
        for k in range(chunk * part, (chunk + 1) * part):
            mix_block(k)

    order = sorted(range(len(steps)), key=lambda h: (-abs(steps[h]), h))
    halo_copies = []
    for h in order:
        picked[h] = product(sent[...], tables[h]).astype(jnp.bfloat16)
        copy = pltpu.make_async_remote_copy(
            src_ref=picked.at[h],
            dst_ref=received.at[h],
            send_sem=halo_send_sem.at[h],
            recv_sem=halo_recv_sem.at[h],
            device_id=(peer(steps[h]),),
            device_id_type=MESH,
        )
        copy.start()
        halo_copies.append(copy)
    ghosts = []
    line = jnp.zeros((1, lanes), jnp.int32)
    for h in range(len(steps)):
        for r in range(depth):
            used = (line + halo_rows[0, h]) > r
            ghosts.append(jnp.where(used, halo_ghost[0, h, r : r + 1, :], -1))
    columns = jnp.transpose(jnp.concatenate(ghosts, axis=0))
    ones = jnp.ones((16, len(ghosts) * lanes), jnp.bfloat16)

    def scatter_cells(index, _):
        base = pl.multiple_of(index * rows, rows)
        run = pl.ds(base, rows)
        ids = lax.broadcasted_iota(jnp.int32, (lanes, rows), 1) + base
        pull = 0.25 * wet[0:1, run].astype(jnp.float32)
        for i in range(len(ghosts)):
            hit = ids == columns[:, i : i + 1]
            scatter[i * lanes : (i + 1) * lanes, run] = jnp.where(hit, pull, 0.0).astype(
                jnp.bfloat16
            )
        keep = 1.0 - product(ones, scatter[:, run])[0:1]
        for t in range(tracers):
            mixed[t, :, run] = keep * mixed[t, :, run]
        return 0

    lax.fori_loop(0, cells // rows, scatter_cells, 0)
    for copy in halo_copies:
        copy.wait()


def halo_kernel(received, scatter, kept, flux_in, flux_out, out):
    tracers, levels, tile = out.shape
    run = pl.ds(pl.multiple_of(pl.program_id(0) * tile, tile), tile)
    values = jnp.concatenate([received[h] for h in range(received.shape[0])], axis=1)
    summed = product(values, scatter[:, run])
    for t in range(tracers):
        out[t] = kept[t, :, run] + summed[t * levels : (t + 1) * levels]
    flux_out[...] = flux_in[...]


def body(
    atm_flux,
    remap_send,
    remap_target,
    remap_counts,
    remap_weights,
    coupling,
    tracer,
    wet,
    mix_inverse,
    halo_send,
    halo_ghost,
    halo_rows,
):
    spans, slots = remap_send.shape[1:]
    block = remap_weights.shape[-1]
    fluxes = atm_flux.shape[0]
    tracers, levels, cells = tracer.shape
    blocks = cells // block
    hosts, depth, lanes = halo_send.shape[1:]
    picks = depth * lanes
    features = tracers * levels
    wet_row = wet.reshape(1, cells)
    vmem = pl.BlockSpec(memory_space=pltpu.VMEM)
    smem = pl.BlockSpec(memory_space=pltpu.SMEM)
    hbm = pl.BlockSpec(memory_space=pltpu.HBM)
    flux, kept, received, scatter = pl.pallas_call(
        couple_kernel,
        out_shape=(
            pltpu.VMEM((fluxes, cells), jnp.float32),
            pltpu.VMEM((tracers, levels, cells), jnp.float32),
            pltpu.VMEM((hosts, features, picks), jnp.bfloat16),
            pltpu.VMEM((hosts * picks, cells), jnp.bfloat16),
        ),
        in_specs=[smem] * 5 + [vmem] * 4 + [hbm] * 3,
        out_specs=(vmem, vmem, vmem, vmem),
        scratch_shapes=[
            pltpu.VMEM((spans, slots, block, block), jnp.bfloat16),
            pltpu.VMEM((tracers, levels, cells), jnp.float32),
            pltpu.VMEM((blocks, levels, levels), jnp.float32),
            pltpu.VMEM((features, cells), jnp.bfloat16),
            pltpu.VMEM((tracers, cells), jnp.float32),
            pltpu.VMEM((blocks * fluxes, block), jnp.float32),
            pltpu.VMEM((spans, slots, fluxes, block), jnp.bfloat16),
            pltpu.VMEM((spans, slots, fluxes, block), jnp.bfloat16),
            pltpu.VMEM((hosts, cells, picks), jnp.bfloat16),
            pltpu.VMEM((hosts, features, picks), jnp.bfloat16),
            pltpu.SemaphoreType.DMA((2 * CHUNKS + 1,)),
            pltpu.SemaphoreType.DMA((spans,)),
            pltpu.SemaphoreType.DMA((spans,)),
            pltpu.SemaphoreType.DMA((hosts,)),
            pltpu.SemaphoreType.DMA((hosts,)),
        ],
        compiler_params=pltpu.CompilerParams(
            collective_id=0, has_side_effects=True, vmem_limit_bytes=50 * 1024 * 1024 + 512 * 1024
        ),
        name="couple",
    )(
        remap_send.transpose(1, 0, 2),
        remap_target.transpose(1, 0, 2),
        remap_counts,
        coupling,
        halo_rows,
        atm_flux,
        wet_row,
        halo_send,
        halo_ghost,
        remap_weights,
        tracer,
        mix_inverse,
    )
    tile = min(TILE, cells)
    return pl.pallas_call(
        halo_kernel,
        grid=(cells // tile,),
        out_shape=(
            jax.ShapeDtypeStruct((fluxes, cells), jnp.float32),
            jax.ShapeDtypeStruct((tracers, levels, cells), jnp.float32),
        ),
        in_specs=[vmem, vmem, vmem, pl.BlockSpec((fluxes, tile), lambda i: (0, i))],
        out_specs=(
            pl.BlockSpec((fluxes, tile), lambda i: (0, i)),
            pl.BlockSpec((tracers, levels, tile), lambda i: (0, 0, i)),
        ),
        compiler_params=pltpu.CompilerParams(vmem_limit_bytes=32 * 1024 * 1024),
        name="halo",
    )(received, scatter, kept, flux)


def solution(mesh):
    return jax.shard_map(
        body,
        mesh=mesh,
        in_specs=(
            P(None, "patch"),
            P("patch", None, None),
            P("patch", None, None),
            P("patch", None),
            P("patch", None, None, None, None),
            P(),
            P(None, None, "patch"),
            P("patch"),
            P("patch", None, None),
            P("patch", None, None, None),
            P("patch", None, None, None),
            P("patch", None),
        ),
        out_specs=(P(None, "patch"), P(None, None, "patch")),
        check_vma=False,
    )
```

profile of v0, /device:TPU:0, one launch (start us, length us, event | category | flops | bytes accessed | tf_op | source)
XLA Modules:
  0.0 33.2 jit_solution(11936339606056823079)
XLA Ops:
  0.6 27.2 %couple.1 = (f32[8,4096]{1,0:T(8,128)S(1)}, f32[2,128,4096]{2,1,0:T(8,128)S(1)}, bf16[4,256,256]{2,1,0:T(8,128)(2,1)S(1)}, bf16[1024,4096]{1,0:T(8,128)(2,1)S(1)}) custom-call(s32[5,1,8]{2,1,0:T(1,128)} %bitcast.4, s32[5,1,8]{2,1,0:T(1,128)} %bitcast.5, s32[1,5]{1,0:T(1,128)} %remap_counts.1, f32[2,8]{1,0:T(2,128)} %coupling.1, s32[1,4]{1,0:T(1,128)} %halo_rows.1, ...), custom_call_target="tpu_custom_call" | custom-call | tf_op jit(solution)/shard_map/couple/pallas_call | solution.py:274
  27.8 5.4 %halo.1 = (f32[8,4096]{1,0:T(8,128)}, f32[2,128,4096]{2,1,0:T(8,128)}) custom-call(bf16[4,256,256]{2,1,0:T(8,128)(2,1)S(1)} %get-tuple-element.6.received, bf16[1024,4096]{1,0:T(8,128)(2,1)S(1)} %get-tuple-element.7.scatter, f32[2,128,4096]{2,1,0:T(8,128)S(1)} %get-tuple-element.8.kept, f32[8,4096]{1,0:T(8,128)S(1)} %get-tuple-element.9.flux_in), custom_call_target="tpu_custom_call" | custom-call | tf_op jit(solution)/shard_map/halo/pallas_call | solution.py:320
where the time goes:
time: 33.4 us; the launch traced here: 33.2 us
  Pallas kernels  32.6 us (98%)
  between operations  0.64 us (2%)
    pallas_call x1, Pallas kernels, body(): pl.pallas_call(couple_kernel, out_shape=(pltpu.VMEM((fluxes, cells), jnp....  27.2 us
    pallas_call x1, Pallas kernels, body(): pl.pallas_call(halo_kernel, grid=(cells // tile,), out_shape=(jax.ShapeDt...  5.44 us

commit v1 on v0

v1 whole, which is shorter than its diff:
```python
import jax
import jax.numpy as jnp
from jax import lax
from jax.experimental import pallas as pl
from jax.experimental.pallas import tpu as pltpu
from jax.sharding import PartitionSpec as P

MESH = pl.DeviceIdType.MESH
CHUNKS = 4
EARLY = 1
TILE = 512


def split(value):
    high = value.astype(jnp.bfloat16)
    return high, (value - high.astype(jnp.float32)).astype(jnp.bfloat16)


def product(left, right):
    return jnp.dot(left, right, preferred_element_type=jnp.float32)


def couple_kernel(
    send_hbm,
    target_hbm,
    counts_hbm,
    coupling_hbm,
    halo_rows_hbm,
    atm_hbm,
    wet_hbm,
    halo_send_hbm,
    halo_ghost_hbm,
    weights_hbm,
    tracer_hbm,
    inverse_hbm,
    flux_out,
    mixed,
    values,
    scatter,
    remap_send,
    remap_target,
    remap_counts,
    coupling,
    halo_rows,
    picks_smem,
    atm,
    atm_blocks,
    wet,
    halo_send,
    halo_ghost,
    weights,
    tracer,
    inverse,
    base_rows,
    gathered,
    surface,
    surface_rows,
    surface_gathered,
    surface_out,
    surface_in,
    total,
    outgoing,
    arrived,
    picked,
    received,
    column,
    tips,
    tips_in,
    cells_in,
    load_sem,
    small_sem,
    flux_send_sem,
    flux_recv_sem,
    halo_send_sem,
    halo_recv_sem,
    side_send_sem,
    side_recv_sem,
):
    size = lax.axis_size("patch")
    me = lax.axis_index("patch")
    spans, slots = remap_send.shape[0], remap_send.shape[2]
    radius = spans // 2
    tracers, levels, cells = tracer.shape
    block = weights.shape[-1]
    blocks = cells // block
    fluxes = atm.shape[0]
    steps = [d - radius for d in range(spans) if d != radius]
    hosts = len(steps)
    depth, lanes = halo_send.shape[1], halo_send.shape[2]
    picks = depth * lanes

    def peer(step):
        return lax.rem(me + step + size, size)
    barrier = pltpu.get_barrier_semaphore()
    for step in steps:
        pl.semaphore_signal(barrier, inc=1, device_id=(peer(step),), device_id_type=MESH)

    small = [
        pltpu.make_async_copy(src, dst, small_sem.at[i])
        for i, (src, dst) in enumerate(
            [
                (send_hbm, remap_send),
                (atm_hbm, atm),
                (wet_hbm, wet),
                (target_hbm, remap_target),
                (counts_hbm, remap_counts),
                (coupling_hbm, coupling),
                (halo_rows_hbm, halo_rows),
                (halo_send_hbm.at[0], picks_smem),
                (halo_send_hbm.at[0], halo_send),
                (halo_ghost_hbm.at[0], halo_ghost),
            ]
        )
    ]
    for copy in small:
        copy.start()
    part, span = blocks // CHUNKS, cells // CHUNKS
    loads = []
    for chunk in range(CHUNKS):
        run = pl.ds(chunk * span, span)
        group = pl.ds(chunk * part, part)
        loads.append(
            pltpu.make_async_copy(inverse_hbm.at[group], inverse.at[group], load_sem.at[2 * chunk])
        )
        loads.append(
            pltpu.make_async_copy(
                tracer_hbm.at[:, :, run], tracer.at[:, :, run], load_sem.at[2 * chunk + 1]
            )
        )
    for load in loads:
        load.start()
    weight_load = pltpu.make_async_copy(weights_hbm.at[0], weights, load_sem.at[2 * CHUNKS])
    weight_load.start()
    for copy in small[:2]:
        copy.wait()
    for a in range(atm_blocks.shape[0]):
        atm_blocks[a] = atm[:, a * block : (a + 1) * block]
    for d in range(spans):
        for c in range(slots):
            piece = atm_blocks[remap_send[d, 0, c]]
            if d == radius:
                arrived[d, c] = piece
            else:
                outgoing[d, c] = piece

    lane = lax.broadcasted_iota(jnp.int32, (levels, block), 1)

    def mix_block(k):
        run = slice(k * block, (k + 1) * block)
        full = inverse[k]
        high, low = split(full)
        awake = wet[0:1, run] != 0
        held = [tracer[t, :, run] for t in range(tracers)]
        right_high, right_low = split(jnp.concatenate(held, axis=1))
        solved = product(
            jnp.concatenate([high, low, high], axis=1),
            jnp.concatenate([right_high, right_high, right_low], axis=0),
        )
        for t in range(tracers):
            value = jnp.where(awake, solved[:, t * block : (t + 1) * block], held[t])
            mixed[t, :, run] = value
            base_rows[t, run, :] = jnp.transpose(value)
        first = jnp.broadcast_to(full[:, 0:1], (levels, block))
        if k % block == 0:
            column[k // block] = first
        else:
            column[k // block] = jnp.where(lane == k % block, first, column[k // block])

    def mix_chunk(chunk):
        loads[2 * chunk].wait()
        loads[2 * chunk + 1].wait()
        for k in range(chunk * part, (chunk + 1) * part):
            mix_block(k)
    small[2].wait()
    for chunk in range(EARLY):
        mix_chunk(chunk)
    pl.semaphore_wait(barrier, len(steps))
    flux_copies = {}
    for step in sorted(steps, key=lambda step: -abs(step)):
        d = step + radius
        flux_copies[d] = pltpu.make_async_remote_copy(
            src_ref=outgoing.at[d],
            dst_ref=arrived.at[d],
            send_sem=flux_send_sem.at[d],
            recv_sem=flux_recv_sem.at[d],
            device_id=(peer(step),),
            device_id_type=MESH,
        )
        flux_copies[d].start()
    for chunk in range(EARLY, CHUNKS):
        mix_chunk(chunk)

    order = [h for h in range(hosts) if steps[h] > 0]
    order += [h for h in range(hosts)[::-1] if steps[h] < 0]

    def remote(source, target, sems, h):
        return pltpu.make_async_remote_copy(
            src_ref=source,
            dst_ref=target.at[h],
            send_sem=sems[0].at[h],
            recv_sem=sems[1].at[h],
            device_id=(peer(steps[h]),),
            device_id_type=MESH,
        )
    for copy in small[3:]:
        copy.wait()
    halo_copies = []
    for h in order:
        for row in range(picks):
            cell = picks_smem[h, row // lanes, row % lanes]
            for t in range(tracers):
                gathered[t, row] = base_rows[t, cell]
        for t in range(tracers):
            picked[h, t * levels : (t + 1) * levels, :] = jnp.transpose(gathered[t]).astype(
                jnp.bfloat16
            )
        copy = remote(picked.at[h], received, (halo_send_sem, halo_recv_sem), h)
        copy.start()
        halo_copies.append(copy)
    flat = jnp.concatenate([jnp.transpose(column[i]) for i in range(column.shape[0])], axis=0)
    tips[...] = flat[:blocks].astype(jnp.bfloat16)
    for h in order:
        for source, target, kind in ((tips, tips_in, 0), (halo_send.at[h], cells_in, 1)):
            copy = remote(source, target, (side_send_sem.at[kind], side_recv_sem.at[kind]), h)
            copy.start()
            halo_copies.append(copy)
    weight_load.wait()
    owner = lax.broadcasted_iota(jnp.int32, (blocks, fluxes, block), 0)
    blank = jnp.zeros((fluxes, block), jnp.int32)
    for copy in flux_copies.values():
        copy.wait_recv()
    for d in range(spans):
        pieces = []
        for c in range(slots):
            used = (blank + remap_counts[0, d]) > c
            piece = jnp.where(used, arrived[d, c].astype(jnp.float32), 0.0)
            placed = jnp.where(owner == remap_target[d, 0, c], piece[None], 0.0)
            pieces.append(placed.reshape(blocks * fluxes, block).astype(jnp.bfloat16))
        left = jnp.concatenate(pieces, axis=1)
        term = product(left, weights[d].reshape(slots * block, block))
        if d == 0:
            total[...] = term
        else:
            total[...] += term
    pad = surface.shape[0] - tracers
    for b in range(blocks):
        run = slice(b * block, (b + 1) * block)
        flux = total[b * fluxes : (b + 1) * fluxes, :] * wet[0:1, run].astype(jnp.float32)
        flux_out[:, run] = flux
        rows = []
        for t in range(tracers):
            value = coupling[t, 0] * flux[0:1, :]
            for f in range(1, fluxes):
                value = value + coupling[t, f] * flux[f : f + 1, :]
            rows.append(value)
        stacked = jnp.concatenate(rows + [jnp.zeros((pad, block), jnp.float32)], axis=0)
        surface[:, run] = stacked
        surface_rows[run, :] = jnp.transpose(stacked)
    for h in order:
        for row in range(picks):
            cell = picks_smem[h, row // lanes, row % lanes]
            surface_gathered[row] = surface_rows[cell]
        surface_out[h] = jnp.transpose(surface_gathered[...])[:tracers]
        copy = remote(surface_out.at[h], surface_in, (side_send_sem.at[2], side_recv_sem.at[2]), h)
        copy.start()
        halo_copies.append(copy)
    ghosts = []
    line = jnp.zeros((1, lanes), jnp.int32)
    for h in range(hosts):
        for r in range(depth):
            used = (line + halo_rows[0, h]) > r
            ghosts.append(jnp.where(used, halo_ghost[h, r : r + 1, :], -1))
    places = jnp.transpose(jnp.concatenate(ghosts, axis=0))
    ones = jnp.ones((16, len(ghosts) * lanes), jnp.bfloat16)
    rows = min(TILE, cells)

    def scatter_cells(index, _):
        base = pl.multiple_of(index * rows, rows)
        run = pl.ds(base, rows)
        ids = lax.broadcasted_iota(jnp.int32, (lanes, rows), 1) + base
        pull = 0.25 * wet[0:1, run].astype(jnp.float32)
        for i in range(len(ghosts)):
            hit = ids == places[:, i : i + 1]
            scatter[i * lanes : (i + 1) * lanes, run] = jnp.where(hit, pull, 0.0).astype(
                jnp.bfloat16
            )
        keep = 1.0 - product(ones, scatter[:, run])[0:1]
        for i in range(rows // block):
            near = pl.ds(pl.multiple_of(base + i * block, block), block)
            first = jnp.broadcast_to(
                inverse[index * (rows // block) + i, :, 0:1], (levels, block)
            )
            for t in range(tracers):
                mixed[t, :, near] = keep[:, i * block : (i + 1) * block] * (
                    mixed[t, :, near] + first * surface[t : t + 1, near]
                )
        return 0
    lax.fori_loop(0, cells // rows, scatter_cells, 0)

    ids = lax.broadcasted_iota(jnp.int32, (blocks, picks), 0)
    shift = block.bit_length() - 1

    def correct(h):
        for source, target, sems in (
            (picked.at[h], received, (halo_send_sem, halo_recv_sem)),
            (tips, tips_in, (side_send_sem.at[0], side_recv_sem.at[0])),
            (halo_send.at[h], cells_in, (side_send_sem.at[1], side_recv_sem.at[1])),
            (surface_out.at[h], surface_in, (side_send_sem.at[2], side_recv_sem.at[2])),
        ):
            remote(source, target, sems, h).wait_recv()
        where = jnp.concatenate([cells_in[h, r : r + 1, :] for r in range(depth)], axis=1)
        hit = ids == lax.shift_right_logical(where, shift)
        first = lax.dot_general(
            tips_in[h],
            jnp.where(hit, 1.0, 0.0).astype(jnp.bfloat16),
            (((0,), (0,)), ((), ())),
            preferred_element_type=jnp.float32,
        )
        for t in range(tracers):
            level = slice(t * levels, (t + 1) * levels)
            value = received[h, level, :].astype(jnp.float32) + first * surface_in[h, t : t + 1, :]
            values[h, level, :] = value.astype(jnp.bfloat16)

    half = hosts // 2
    for h in range(half)[::-1]:
        correct(h)

    left = jnp.concatenate([values[h] for h in range(half)], axis=1)
    for index in range(cells // rows):
        run = slice(index * rows, (index + 1) * rows)
        summed = product(left, scatter[: half * picks, run])
        for t in range(tracers):
            mixed[t, :, run] += summed[t * levels : (t + 1) * levels]
    for h in range(half, hosts):
        correct(h)
    for copy in list(flux_copies.values()) + halo_copies:
        copy.wait_send()


def halo_kernel(values, scatter, kept, flux_in, flux_out, out):
    tracers, levels, tile = out.shape
    hosts, _, picks = values.shape
    half = hosts // 2
    run = pl.ds(pl.multiple_of(pl.program_id(0) * tile, tile), tile)
    left = jnp.concatenate([values[h] for h in range(half, hosts)], axis=1)
    summed = product(left, scatter[half * picks :, run])
    for t in range(tracers):
        out[t] = kept[t, :, run] + summed[t * levels : (t + 1) * levels]
    flux_out[...] = flux_in[...]


def body(
    atm_flux,
    remap_send,
    remap_target,
    remap_counts,
    remap_weights,
    coupling,
    tracer,
    wet,
    mix_inverse,
    halo_send,
    halo_ghost,
    halo_rows,
):
    spans, slots = remap_send.shape[1:]
    block = remap_weights.shape[-1]
    fluxes = atm_flux.shape[0]
    tracers, levels, cells = tracer.shape
    blocks = cells // block
    hosts, depth, lanes = halo_send.shape[1:]
    picks = depth * lanes
    features = tracers * levels
    lead = -(-tracers // 8) * 8
    vmem = pl.BlockSpec(memory_space=pltpu.VMEM)
    hbm = pl.BlockSpec(memory_space=pltpu.HBM)
    dma = pltpu.SemaphoreType.DMA
    flux, kept, values, scatter = pl.pallas_call(
        couple_kernel,
        out_shape=(
            pltpu.VMEM((fluxes, cells), jnp.float32),
            pltpu.VMEM((tracers, levels, cells), jnp.float32),
            pltpu.VMEM((hosts, features, picks), jnp.bfloat16),
            pltpu.VMEM((hosts * picks, cells), jnp.bfloat16),
        ),
        in_specs=[hbm] * 12,
        out_specs=(vmem, vmem, vmem, vmem),
        scratch_shapes=[
            pltpu.SMEM((spans, 1, slots), jnp.int32),
            pltpu.SMEM((spans, 1, slots), jnp.int32),
            pltpu.SMEM((1, spans), jnp.int32),
            pltpu.SMEM((tracers, fluxes), jnp.float32),
            pltpu.SMEM((1, hosts), jnp.int32),
            pltpu.SMEM((hosts, depth, lanes), jnp.int32),
            pltpu.VMEM(atm_flux.shape, jnp.bfloat16),
            pltpu.VMEM((atm_flux.shape[1] // block, fluxes, block), jnp.bfloat16),
            pltpu.VMEM((1, cells), jnp.int32),
            pltpu.VMEM((hosts, depth, lanes), jnp.int32),
            pltpu.VMEM((hosts, depth, lanes), jnp.int32),
            pltpu.VMEM((spans, slots, block, block), jnp.bfloat16),
            pltpu.VMEM((tracers, levels, cells), jnp.float32),
            pltpu.VMEM((blocks, levels, levels), jnp.float32),
            pltpu.VMEM((tracers, cells, levels), jnp.float32),
            pltpu.VMEM((tracers, picks, levels), jnp.float32),
            pltpu.VMEM((lead, cells), jnp.float32),
            pltpu.VMEM((cells, lead), jnp.float32),
            pltpu.VMEM((picks, lead), jnp.float32),
            pltpu.VMEM((hosts, tracers, picks), jnp.float32),
            pltpu.VMEM((hosts, tracers, picks), jnp.float32),
            pltpu.VMEM((blocks * fluxes, block), jnp.float32),
            pltpu.VMEM((spans, slots, fluxes, block), jnp.bfloat16),
            pltpu.VMEM((spans, slots, fluxes, block), jnp.bfloat16),
            pltpu.VMEM((hosts, features, picks), jnp.bfloat16),
            pltpu.VMEM((hosts, features, picks), jnp.bfloat16),
            pltpu.VMEM((-(-blocks // block), levels, block), jnp.float32),
            pltpu.VMEM((blocks, levels), jnp.bfloat16),
            pltpu.VMEM((hosts, blocks, levels), jnp.bfloat16),
            pltpu.VMEM((hosts, depth, lanes), jnp.int32),
            dma((2 * CHUNKS + 1,)),
            dma((10,)),
            dma((spans,)),
            dma((spans,)),
            dma((hosts,)),
            dma((hosts,)),
            dma((3, hosts)),
            dma((3, hosts)),
        ],
        compiler_params=pltpu.CompilerParams(
            collective_id=0, has_side_effects=True, vmem_limit_bytes=48 * 1024 * 1024
        ),
        name="couple",
    )(
        remap_send.transpose(1, 0, 2),
        remap_target.transpose(1, 0, 2),
        remap_counts,
        coupling,
        halo_rows,
        atm_flux,
        wet.reshape(1, cells),
        halo_send,
        halo_ghost,
        remap_weights,
        tracer,
        mix_inverse,
    )
    tile = min(TILE, cells)
    return pl.pallas_call(
        halo_kernel,
        grid=(cells // tile,),
        out_shape=(
            jax.ShapeDtypeStruct((fluxes, cells), jnp.float32),
            jax.ShapeDtypeStruct((tracers, levels, cells), jnp.float32),
        ),
        in_specs=[vmem, vmem, vmem, pl.BlockSpec((fluxes, tile), lambda i: (0, i))],
        out_specs=(
            pl.BlockSpec((fluxes, tile), lambda i: (0, i)),
            pl.BlockSpec((tracers, levels, tile), lambda i: (0, 0, i)),
        ),
        compiler_params=pltpu.CompilerParams(vmem_limit_bytes=32 * 1024 * 1024),
        name="halo",
    )(values, scatter, kept, flux)


def solution(mesh):
    return jax.shard_map(
        body,
        mesh=mesh,
        in_specs=(
            P(None, "patch"),
            P("patch", None, None),
            P("patch", None, None),
            P("patch", None),
            P("patch", None, None, None, None),
            P(),
            P(None, None, "patch"),
            P("patch"),
            P("patch", None, None),
            P("patch", None, None, None),
            P("patch", None, None, None),
            P("patch", None),
        ),
        out_specs=(P(None, "patch"), P(None, None, "patch")),
        check_vma=False,
    )
```

time: 33.4 us -> 26 us (0.78)
  Pallas kernels: 32.6 us -> 25 us
    pallas_call x1, Pallas kernels: 27.2 us -> 20.2 us  [body(): pl.pallas_call(couple_kernel, out_shape=(pltpu.VMEM((fluxes, cells), jnp....]
    pallas_call x1, Pallas kernels: 5.44 us -> 4.74 us  [body(): pl.pallas_call(halo_kernel, grid=(cells // tile,), out_shape=(jax.ShapeDt...]
where the time goes in v1:
time: 26 us; the launch traced here: 25.6 us
  Pallas kernels  25 us (96%)
  between operations  0.64 us (2%)
    pallas_call x1, Pallas kernels, body(): pl.pallas_call(couple_kernel, out_shape=(pltpu.VMEM((fluxes, cells), jnp....  20.2 us
    pallas_call x1, Pallas kernels, body(): pl.pallas_call(halo_kernel, grid=(cells // tile,), out_shape=(jax.ShapeDt...  4.74 us

profile of v1, /device:TPU:0, one launch (start us, length us, event | category | flops | bytes accessed | tf_op | source)
XLA Modules:
  0.0 25.6 jit_solution(1877016169101771235)
XLA Ops:
  0.6 20.2 %couple.1 = (f32[8,4096]{1,0:T(8,128)S(1)}, f32[2,128,4096]{2,1,0:T(8,128)S(1)}, bf16[4,256,256]{2,1,0:T(8,128)(2,1)S(1)}, bf16[1024,4096]{1,0:T(8,128)(2,1)S(1)}) custom-call(s32[5,1,8]{2,1,0:T(1,128)} %bitcast.4, s32[5,1,8]{2,1,0:T(1,128)} %bitcast.5, s32[1,5]{1,0:T(1,128)} %counts_hbm.1, f32[2,8]{1,0:T(2,128)} %coupling_hbm.1, s32[1,4]{1,0:T(1,128)} %halo_rows_hbm.1, ...), custom_call_target="tpu_custom_call" | custom-call | tf_op jit(solution)/shard_map/couple/pallas_call | solution.py:378
  20.9 4.7 %halo.1 = (f32[8,4096]{1,0:T(8,128)}, f32[2,128,4096]{2,1,0:T(8,128)}) custom-call(bf16[4,256,256]{2,1,0:T(8,128)(2,1)S(1)} %get-tuple-element.6.values, bf16[1024,4096]{1,0:T(8,128)(2,1)S(1)} %get-tuple-element.7.scatter, f32[2,128,4096]{2,1,0:T(8,128)S(1)} %get-tuple-element.8.kept, f32[8,4096]{1,0:T(8,128)S(1)} %get-tuple-element.9.flux_in), custom_call_target="tpu_custom_call" | custom-call | tf_op jit(solution)/shard_map/halo/pallas_call | solution.py:447

commit v2 on v1

v2 whole, which is shorter than its diff:
```python
import jax
import jax.numpy as jnp
from jax import lax
from jax.experimental import pallas as pl
from jax.experimental.pallas import tpu as pltpu
from jax.sharding import PartitionSpec as P

MESH = pl.DeviceIdType.MESH
CHUNKS = 4
TILE = 512


def split(value):
    high = value.astype(jnp.bfloat16)
    return high, (value - high.astype(jnp.float32)).astype(jnp.bfloat16)


def product(left, right):
    return jnp.dot(left, right, preferred_element_type=jnp.float32)


def couple_kernel(
    send_hbm,
    target_hbm,
    counts_hbm,
    coupling_hbm,
    halo_rows_hbm,
    atm_hbm,
    wet_hbm,
    halo_send_hbm,
    halo_ghost_hbm,
    weights_hbm,
    tracer_hbm,
    inverse_hbm,
    flux_out,
    mixed,
    values,
    scatter,
    remap_send,
    remap_target,
    remap_counts,
    coupling,
    halo_rows,
    picks_smem,
    atm,
    atm_blocks,
    wet,
    halo_send,
    halo_ghost,
    weights,
    tracer,
    inverse,
    base_rows,
    gathered,
    factor,
    keep,
    surface,
    surface_rows,
    surface_gathered,
    surface_out,
    surface_in,
    total,
    outgoing,
    arrived,
    picked,
    received,
    column,
    tips,
    tips_in,
    cells_in,
    load_sem,
    small_sem,
    flux_send_sem,
    flux_recv_sem,
    halo_send_sem,
    halo_recv_sem,
    side_send_sem,
    side_recv_sem,
):
    size = lax.axis_size("patch")
    me = lax.axis_index("patch")
    spans, slots = remap_send.shape[0], remap_send.shape[2]
    radius = spans // 2
    tracers, levels, cells = tracer.shape
    block = weights.shape[-1]
    blocks = cells // block
    fluxes = atm.shape[0]
    steps = [d - radius for d in range(spans) if d != radius]
    hosts = len(steps)
    depth, lanes = halo_send.shape[1], halo_send.shape[2]
    picks = depth * lanes

    def peer(step):
        return lax.rem(me + step + size, size)
    barrier = pltpu.get_barrier_semaphore()
    for step in steps:
        pl.semaphore_signal(barrier, inc=1, device_id=(peer(step),), device_id_type=MESH)

    small = [
        pltpu.make_async_copy(src, dst, small_sem.at[i])
        for i, (src, dst) in enumerate(
            [
                (send_hbm, remap_send),
                (atm_hbm, atm),
                (wet_hbm, wet),
                (target_hbm, remap_target),
                (counts_hbm, remap_counts),
                (coupling_hbm, coupling),
                (halo_rows_hbm, halo_rows),
                (halo_send_hbm.at[0], picks_smem),
                (halo_send_hbm.at[0], halo_send),
                (halo_ghost_hbm.at[0], halo_ghost),
            ]
        )
    ]
    for copy in small:
        copy.start()
    part, span = blocks // CHUNKS, cells // CHUNKS
    loads = {}
    for t in range(tracers):
        for chunk in range(CHUNKS):
            run = pl.ds(chunk * span, span)
            bunch = pl.ds(chunk * part, part)
            if t == 0:
                loads[chunk] = pltpu.make_async_copy(
                    inverse_hbm.at[bunch], inverse.at[bunch], load_sem.at[chunk]
                )
                loads[chunk].start()
            loads[t, chunk] = pltpu.make_async_copy(
                tracer_hbm.at[t, :, run],
                tracer.at[t, :, run],
                load_sem.at[(1 + t) * CHUNKS + chunk],
            )
            loads[t, chunk].start()
    weight_load = pltpu.make_async_copy(weights_hbm.at[0], weights, load_sem.at[(1 + tracers) * CHUNKS])
    weight_load.start()
    for copy in small[:2]:
        copy.wait()
    for a in range(atm_blocks.shape[0]):
        atm_blocks[a] = atm[:, a * block : (a + 1) * block]
    for d in range(spans):
        for c in range(slots):
            piece = atm_blocks[remap_send[d, 0, c]]
            if d == radius:
                arrived[d, c] = piece
            else:
                outgoing[d, c] = piece

    low = me < radius
    order = [h for h in range(hosts) if steps[h] > 0]
    order += [h for h in range(hosts)[::-1] if steps[h] < 0]

    def remote(source, target, sems, index, h):
        return pltpu.make_async_remote_copy(
            src_ref=source,
            dst_ref=target,
            send_sem=sems[0].at[index],
            recv_sem=sems[1].at[index],
            device_id=(peer(steps[h]),),
            device_id_type=MESH,
        )

    def flux_copy(h):
        d = steps[h] + radius
        return remote(outgoing.at[d], arrived.at[d], (flux_send_sem, flux_recv_sem), h, h)

    def row_copy(h, t):
        level = pl.ds(t * levels, levels)
        return remote(
            picked.at[h, level], received.at[h, level], (halo_send_sem, halo_recv_sem), (h, t), h
        )

    def side_copy(h, kind):
        source, target = (
            (tips, tips_in.at[h]),
            (halo_send.at[h], cells_in.at[h]),
            (surface_out.at[h], surface_in.at[h]),
        )[kind]
        return remote(source, target, (side_send_sem, side_recv_sem), (kind, h), h)

    def enter():
        pl.semaphore_wait(barrier, len(steps))
        for h in sorted(range(hosts), key=lambda h: -abs(steps[h])):
            flux_copy(h).start()

    lane = lax.broadcasted_iota(jnp.int32, (levels, block), 1)

    def mix_block(k, t):
        run = slice(k * block, (k + 1) * block)
        if t == 0:
            full = inverse[k]
            high, low_part = split(full)
            left = jnp.concatenate([high, low_part, high], axis=1)
            factor[k] = left
            first = jnp.broadcast_to(full[:, 0:1], (levels, block))
            if k % block == 0:
                column[k // block] = first
            else:
                column[k // block] = jnp.where(lane == k % block, first, column[k // block])
        else:
            left = factor[k]
        held = tracer[t, :, run]
        right_high, right_low = split(held)
        solved = product(left, jnp.concatenate([right_high, right_high, right_low], axis=0))
        value = jnp.where(wet[0:1, run] != 0, solved, held)
        mixed[t, :, run] = value
        base_rows[t, run, :] = jnp.transpose(value)

    def mix_chunk(chunk, t):
        if t == 0:
            loads[chunk].wait()
        loads[t, chunk].wait()
        for k in range(chunk * part, (chunk + 1) * part):
            mix_block(k, t)
    small[2].wait()
    mix_chunk(0, 0)

    @pl.when(jnp.logical_not(low))
    def _():
        enter()

    for chunk in range(1, CHUNKS):
        mix_chunk(chunk, 0)
    for copy in small[3:]:
        copy.wait()
    held_back = [(h, tracers - 1) for h in order if steps[h] < 0]
    flat = jnp.concatenate([jnp.transpose(column[i]) for i in range(column.shape[0])], axis=0)
    tips[...] = flat[:blocks].astype(jnp.bfloat16)
    sent = []
    for t in range(tracers):
        if t > 0:
            for chunk in range(CHUNKS):
                mix_chunk(chunk, t)
        for h in order:
            for row in range(picks):
                cell = picks_smem[h, row // lanes, row % lanes]
                gathered[row] = base_rows[t, cell]
            picked[h, t * levels : (t + 1) * levels, :] = jnp.transpose(gathered[...]).astype(
                jnp.bfloat16
            )
            bundle = [row_copy(h, t)] if (h, t) not in held_back else []
            if t == 0:
                bundle += [side_copy(h, 0), side_copy(h, 1)]
            sent += bundle

            @pl.when(jnp.logical_not(low))
            def _():
                for copy in bundle:
                    copy.start()

    @pl.when(low)
    def _():
        enter()
        for copy in sent:
            copy.start()
    ghosts = []
    line = jnp.zeros((1, lanes), jnp.int32)
    for h in range(hosts):
        for r in range(depth):
            used = (line + halo_rows[0, h]) > r
            ghosts.append(jnp.where(used, halo_ghost[h, r : r + 1, :], -1))
    places = jnp.transpose(jnp.concatenate(ghosts, axis=0))
    rows = min(TILE, cells)
    ones = jnp.ones((16, len(ghosts) * lanes), jnp.bfloat16)
    marks = [
        jnp.broadcast_to(places[:, i : i + 1], (lanes, rows)).astype(jnp.int16)
        for i in range(len(ghosts))
    ]
    ids = lax.broadcasted_iota(jnp.int32, (lanes, rows), 1).astype(jnp.int16)
    for index in range(cells // rows):
        run = slice(index * rows, (index + 1) * rows)
        pull = jnp.broadcast_to(0.25 * wet[0:1, run].astype(jnp.float32), (lanes, rows)).astype(
            jnp.bfloat16
        )
        here = ids + jnp.int16(index * rows)
        for i in range(len(ghosts)):
            scatter[i * lanes : (i + 1) * lanes, run] = jnp.where(
                here == marks[i], pull, jnp.bfloat16(0)
            )
        keep[:, run] = 1.0 - product(ones, scatter[:, run])[0:1]
    weight_load.wait()
    owner = lax.broadcasted_iota(jnp.int32, (blocks, fluxes, block), 0)
    blank = jnp.zeros((fluxes, block), jnp.int32)
    for h in range(hosts):
        flux_copy(h).wait_recv()
    for d in range(spans):
        pieces = []
        for c in range(slots):
            used = (blank + remap_counts[0, d]) > c
            piece = jnp.where(used, arrived[d, c].astype(jnp.float32), 0.0)
            placed = jnp.where(owner == remap_target[d, 0, c], piece[None], 0.0)
            pieces.append(placed.reshape(blocks * fluxes, block).astype(jnp.bfloat16))
        left = jnp.concatenate(pieces, axis=1)
        term = product(left, weights[d].reshape(slots * block, block))
        if d == 0:
            total[...] = term
        else:
            total[...] += term
    pad = surface.shape[0] - tracers
    for b in range(blocks):
        run = slice(b * block, (b + 1) * block)
        flux = total[b * fluxes : (b + 1) * fluxes, :] * wet[0:1, run].astype(jnp.float32)
        flux_out[:, run] = flux
        rows = []
        for t in range(tracers):
            value = coupling[t, 0] * flux[0:1, :]
            for f in range(1, fluxes):
                value = value + coupling[t, f] * flux[f : f + 1, :]
            rows.append(value)
        stacked = jnp.concatenate(rows + [jnp.zeros((pad, block), jnp.float32)], axis=0)
        surface[:, run] = stacked
        surface_rows[run, :] = jnp.transpose(stacked)
    for h in order:
        for row in range(picks):
            cell = picks_smem[h, row // lanes, row % lanes]
            surface_gathered[row] = surface_rows[cell]
        surface_out[h] = jnp.transpose(surface_gathered[...])[:tracers]
        side_copy(h, 2).start()
    for h, t in held_back:
        row_copy(h, t).start()
    for k in range(blocks):
        run = slice(k * block, (k + 1) * block)
        first = jnp.broadcast_to(inverse[k, :, 0:1], (levels, block))
        for t in range(tracers):
            mixed[t, :, run] = keep[:, run] * (
                mixed[t, :, run] + first * surface[t : t + 1, run]
            )

    ids = lax.broadcasted_iota(jnp.int32, (blocks, picks), 0)
    shift = block.bit_length() - 1

    def correct(h):
        for kind in range(3):
            side_copy(h, kind).wait_recv()
        for t in range(tracers):
            row_copy(h, t).wait_recv()
        where = jnp.concatenate([cells_in[h, r : r + 1, :] for r in range(depth)], axis=1)
        hit = ids == lax.shift_right_logical(where, shift)
        first = lax.dot_general(
            tips_in[h],
            jnp.where(hit, 1.0, 0.0).astype(jnp.bfloat16),
            (((0,), (0,)), ((), ())),
            preferred_element_type=jnp.float32,
        )
        for t in range(tracers):
            level = slice(t * levels, (t + 1) * levels)
            value = received[h, level, :].astype(jnp.float32) + first * surface_in[h, t : t + 1, :]
            values[level, h * picks : (h + 1) * picks] = value.astype(jnp.bfloat16)

    for h in order:
        correct(h)
    for h in range(hosts):
        flux_copy(h).wait_send()
        for t in range(tracers):
            row_copy(h, t).wait_send()
        for kind in range(3):
            side_copy(h, kind).wait_send()


def halo_kernel(values, scatter, kept, flux_in, flux_out, out, stage, sems):
    tracers, levels, cells = out.shape
    flux_copy = pltpu.make_async_copy(flux_in, flux_out, sems.at[0])
    flux_copy.start()
    tile = min(TILE, cells)
    copies = [flux_copy]
    for index in range(cells // tile):
        run = slice(index * tile, (index + 1) * tile)
        summed = product(values[...], scatter[:, run])
        for t in range(tracers):
            stage[t, :, run] = kept[t, :, run] + summed[t * levels : (t + 1) * levels]
        area = pl.ds(index * tile, tile)
        copy = pltpu.make_async_copy(
            stage.at[:, :, area], out.at[:, :, area], sems.at[1 + index]
        )
        copy.start()
        copies.append(copy)
    for copy in copies:
        copy.wait()


def body(
    atm_flux,
    remap_send,
    remap_target,
    remap_counts,
    remap_weights,
    coupling,
    tracer,
    wet,
    mix_inverse,
    halo_send,
    halo_ghost,
    halo_rows,
):
    spans, slots = remap_send.shape[1:]
    block = remap_weights.shape[-1]
    fluxes = atm_flux.shape[0]
    tracers, levels, cells = tracer.shape
    blocks = cells // block
    hosts, depth, lanes = halo_send.shape[1:]
    picks = depth * lanes
    features = tracers * levels
    lead = -(-tracers // 8) * 8
    vmem = pl.BlockSpec(memory_space=pltpu.VMEM)
    hbm = pl.BlockSpec(memory_space=pltpu.HBM)
    dma = pltpu.SemaphoreType.DMA
    flux, kept, values, scatter = pl.pallas_call(
        couple_kernel,
        out_shape=(
            pltpu.VMEM((fluxes, cells), jnp.float32),
            pltpu.VMEM((tracers, levels, cells), jnp.float32),
            pltpu.VMEM((features, hosts * picks), jnp.bfloat16),
            pltpu.VMEM((hosts * picks, cells), jnp.bfloat16),
        ),
        in_specs=[hbm] * 12,
        out_specs=(vmem, vmem, vmem, vmem),
        scratch_shapes=[
            pltpu.SMEM((spans, 1, slots), jnp.int32),
            pltpu.SMEM((spans, 1, slots), jnp.int32),
            pltpu.SMEM((1, spans), jnp.int32),
            pltpu.SMEM((tracers, fluxes), jnp.float32),
            pltpu.SMEM((1, hosts), jnp.int32),
            pltpu.SMEM((hosts, depth, lanes), jnp.int32),
            pltpu.VMEM(atm_flux.shape, jnp.bfloat16),
            pltpu.VMEM((atm_flux.shape[1] // block, fluxes, block), jnp.bfloat16),
            pltpu.VMEM((1, cells), jnp.int32),
            pltpu.VMEM((hosts, depth, lanes), jnp.int32),
            pltpu.VMEM((hosts, depth, lanes), jnp.int32),
            pltpu.VMEM((spans, slots, block, block), jnp.bfloat16),
            pltpu.VMEM((tracers, levels, cells), jnp.float32),
            pltpu.VMEM((blocks, levels, levels), jnp.float32),
            pltpu.VMEM((tracers, cells, levels), jnp.float32),
            pltpu.VMEM((picks, levels), jnp.float32),
            pltpu.VMEM((blocks, levels, 3 * levels), jnp.bfloat16),
            pltpu.VMEM((1, cells), jnp.float32),
            pltpu.VMEM((lead, cells), jnp.float32),
            pltpu.VMEM((cells, lead), jnp.float32),
            pltpu.VMEM((picks, lead), jnp.float32),
            pltpu.VMEM((hosts, tracers, picks), jnp.float32),
            pltpu.VMEM((hosts, tracers, picks), jnp.float32),
            pltpu.VMEM((blocks * fluxes, block), jnp.float32),
            pltpu.VMEM((spans, slots, fluxes, block), jnp.bfloat16),
            pltpu.VMEM((spans, slots, fluxes, block), jnp.bfloat16),
            pltpu.VMEM((hosts, features, picks), jnp.bfloat16),
            pltpu.VMEM((hosts, features, picks), jnp.bfloat16),
            pltpu.VMEM((-(-blocks // block), levels, block), jnp.float32),
            pltpu.VMEM((blocks, levels), jnp.bfloat16),
            pltpu.VMEM((hosts, blocks, levels), jnp.bfloat16),
            pltpu.VMEM((hosts, depth, lanes), jnp.int32),
            dma(((1 + tracers) * CHUNKS + 1,)),
            dma((10,)),
            dma((hosts,)),
            dma((hosts,)),
            dma((hosts, tracers)),
            dma((hosts, tracers)),
            dma((3, hosts)),
            dma((3, hosts)),
        ],
        compiler_params=pltpu.CompilerParams(
            collective_id=0, has_side_effects=True, vmem_limit_bytes=48 * 1024 * 1024
        ),
        name="couple",
    )(
        remap_send.transpose(1, 0, 2),
        remap_target.transpose(1, 0, 2),
        remap_counts,
        coupling,
        halo_rows,
        atm_flux,
        wet.reshape(1, cells),
        halo_send,
        halo_ghost,
        remap_weights,
        tracer,
        mix_inverse,
    )
    tile = min(TILE, cells)
    return pl.pallas_call(
        halo_kernel,
        out_shape=(
            jax.ShapeDtypeStruct((fluxes, cells), jnp.float32),
            jax.ShapeDtypeStruct((tracers, levels, cells), jnp.float32),
        ),
        in_specs=[vmem] * 4,
        out_specs=(hbm, hbm),
        scratch_shapes=[
            pltpu.VMEM((tracers, levels, cells), jnp.float32),
            dma((1 + cells // tile,)),
        ],
        compiler_params=pltpu.CompilerParams(vmem_limit_bytes=24 * 1024 * 1024),
        name="halo",
    )(values, scatter, kept, flux)


def solution(mesh):
    return jax.shard_map(
        body,
        mesh=mesh,
        in_specs=(
            P(None, "patch"),
            P("patch", None, None),
            P("patch", None, None),
            P("patch", None),
            P("patch", None, None, None, None),
            P(),
            P(None, None, "patch"),
            P("patch"),
            P("patch", None, None),
            P("patch", None, None, None),
            P("patch", None, None, None),
            P("patch", None),
        ),
        out_specs=(P(None, "patch"), P(None, None, "patch")),
        check_vma=False,
    )
```

time: 26 us -> 24.4 us (0.938); the launches traced: 25.6 us -> 24.3 us
  Pallas kernels: 25 us -> 23.6 us
    pallas_call x1, Pallas kernels: 4.74 us -> 3.21 us  [body(): pl.pallas_call(halo_kernel, out_shape=(jax.ShapeDtypeStruct((fluxes, cell...]
where the time goes in v2:
time: 24.4 us; the launch traced here: 24.3 us
  Pallas kernels  23.6 us (97%)
  between operations  0.64 us (3%)
    pallas_call x1, Pallas kernels, body(): pl.pallas_call(couple_kernel, out_shape=(pltpu.VMEM((fluxes, cells), jnp....  20.4 us
    pallas_call x1, Pallas kernels, body(): pl.pallas_call(halo_kernel, out_shape=(jax.ShapeDtypeStruct((fluxes, cell...  3.21 us

profile of v2, /device:TPU:0, one launch (start us, length us, event | category | flops | bytes accessed | tf_op | source)
XLA Modules:
  0.0 24.3 jit_solution(13869720805701356477)
XLA Ops:
  0.6 20.4 %couple.1 = (f32[8,4096]{1,0:T(8,128)S(1)}, f32[2,128,4096]{2,1,0:T(8,128)S(1)}, bf16[256,1024]{1,0:T(8,128)(2,1)S(1)}, bf16[1024,4096]{1,0:T(8,128)(2,1)S(1)}) custom-call(s32[5,1,8]{2,1,0:T(1,128)} %bitcast.4, s32[5,1,8]{2,1,0:T(1,128)} %bitcast.5, s32[1,5]{1,0:T(1,128)} %counts_hbm.1, f32[2,8]{1,0:T(2,128)} %coupling_hbm.1, s32[1,4]{1,0:T(1,128)} %halo_rows_hbm.1, ...), custom_call_target="tpu_custom_call" | custom-call | tf_op jit(solution)/shard_map/couple/pallas_call | solution.py:407
  21.1 3.2 %halo.1 = (f32[8,4096]{1,0:T(8,128)}, f32[2,128,4096]{2,1,0:T(8,128)}) custom-call(bf16[256,1024]{1,0:T(8,128)(2,1)S(1)} %get-tuple-element.6.values, bf16[1024,4096]{1,0:T(8,128)(2,1)S(1)} %get-tuple-element.7.scatter, f32[2,128,4096]{2,1,0:T(8,128)S(1)} %get-tuple-element.8.kept, f32[8,4096]{1,0:T(8,128)S(1)} %get-tuple-element.9.flux_in), custom_call_target="tpu_custom_call" | custom-call | tf_op jit(solution)/shard_map/halo/pallas_call | solution.py:478

commit v3 on v2

--- a/solution.py
+++ b/solution.py
@@ -1,3 +1,5 @@
+import functools
+
 import jax
 import jax.numpy as jnp
 from jax import lax
@@ -6,7 +8,7 @@
 from jax.sharding import PartitionSpec as P
 
 MESH = pl.DeviceIdType.MESH
-CHUNKS = 4
+CHUNKS = 2
 TILE = 512
 
 
@@ -52,6 +54,7 @@
     inverse,
     base_rows,
     gathered,
+    early_values,
     factor,
     keep,
     surface,
@@ -76,6 +79,7 @@
     halo_recv_sem,
     side_send_sem,
     side_recv_sem,
+    ready,
 ):
     size = lax.axis_size("patch")
     me = lax.axis_index("patch")
@@ -117,7 +121,8 @@
         copy.start()
     part, span = blocks // CHUNKS, cells // CHUNKS
     loads = {}
-    for t in range(tracers):
+
+    def load(t):
         for chunk in range(CHUNKS):
             run = pl.ds(chunk * span, span)
             bunch = pl.ds(chunk * part, part)
@@ -132,8 +137,11 @@
                 load_sem.at[(1 + t) * CHUNKS + chunk],
             )
             loads[t, chunk].start()
-    weight_load = pltpu.make_async_copy(weights_hbm.at[0], weights, load_sem.at[(1 + tracers) * CHUNKS])
-    weight_load.start()
+
+    load(0)
+    weight_load = pltpu.make_async_copy(
+        weights_hbm.at[0], weights, load_sem.at[(1 + tracers) * CHUNKS]
+    )
     for copy in small[:2]:
         copy.wait()
     for a in range(atm_blocks.shape[0]):
@@ -146,6 +154,9 @@
             else:
                 outgoing[d, c] = piece
 
+    for t in range(1, tracers):
+        load(t)
+    weight_load.start()
     low = me < radius
     order = [h for h in range(hosts) if steps[h] > 0]
     order += [h for h in range(hosts)[::-1] if steps[h] < 0]
@@ -178,10 +189,24 @@
         )[kind]
         return remote(source, target, (side_send_sem, side_recv_sem), (kind, h), h)
 
-    def enter():
+    far_first = sorted(range(hosts), key=lambda h: -abs(steps[h]))
+    ahead = [h for h in range(hosts) if steps[h] > 0]
+
+    @pl.when(jnp.logical_not(low))
+    def _():
         pl.semaphore_wait(barrier, len(steps))
-        for h in sorted(range(hosts), key=lambda h: -abs(steps[h])):
+        for h in far_first:
             flux_copy(h).start()
+        for h in ahead:
+
+            @pl.when(me - steps[h] < radius)
+            def _():
+                pl.semaphore_signal(
+                    ready.at[h],
+                    inc=1,
+                    device_id=(peer(-steps[h]),),
+                    device_id_type=MESH,
+                )
 
     lane = lax.broadcasted_iota(jnp.int32, (levels, block), 1)
 
@@ -205,32 +230,25 @@
         value = jnp.where(wet[0:1, run] != 0, solved, held)
         mixed[t, :, run] = value
         base_rows[t, run, :] = jnp.transpose(value)
-
-    def mix_chunk(chunk, t):
-        if t == 0:
-            loads[chunk].wait()
-        loads[t, chunk].wait()
+    small[2].wait()
+    for chunk in range(CHUNKS):
+        loads[chunk].wait()
+        loads[0, chunk].wait()
         for k in range(chunk * part, (chunk + 1) * part):
-            mix_block(k, t)
-    small[2].wait()
-    mix_chunk(0, 0)
-
-    @pl.when(jnp.logical_not(low))
-    def _():
-        enter()
-
-    for chunk in range(1, CHUNKS):
-        mix_chunk(chunk, 0)
+            mix_block(k, 0)
     for copy in small[3:]:
         copy.wait()
     held_back = [(h, tracers - 1) for h in order if steps[h] < 0]
     flat = jnp.concatenate([jnp.transpose(column[i]) for i in range(column.shape[0])], axis=0)
     tips[...] = flat[:blocks].astype(jnp.bfloat16)
-    sent = []
+    sent = {h: [] for h in range(hosts)}
+    unsent = {}
     for t in range(tracers):
         if t > 0:
             for chunk in range(CHUNKS):
-                mix_chunk(chunk, t)
+                loads[t, chunk].wait()
+            for k in range(blocks):
+                mix_block(k, t)
         for h in order:
             for row in range(picks):
                 cell = picks_smem[h, row // lanes, row % lanes]
@@ -241,18 +259,89 @@
             bundle = [row_copy(h, t)] if (h, t) not in held_back else []
             if t == 0:
                 bundle += [side_copy(h, 0), side_copy(h, 1)]
-            sent += bundle
-
-            @pl.when(jnp.logical_not(low))
+            go = jnp.logical_not(low)
+            if h in ahead and t == 0:
+                near = jnp.logical_and(low, me + steps[h] >= radius)
+
+                @pl.when(near)
+                def _():
+                    pl.semaphore_wait(ready.at[h], 1)
+                    flux_copy(h).start()
+
+                go = jnp.logical_or(go, near)
+
+            @pl.when(go)
             def _():
                 for copy in bundle:
                     copy.start()
 
+            if h not in ahead or t > 0:
+                sent[h] += bundle
+            else:
+                unsent[h] = bundle
+
     @pl.when(low)
     def _():
-        enter()
-        for copy in sent:
-            copy.start()
+        pl.semaphore_wait(barrier, len(steps))
+        for h in far_first:
+            if h in ahead:
+
+                @pl.when(me + steps[h] < radius)
+                def _():
+                    flux_copy(h).start()
+                    for copy in unsent[h]:
+                        copy.start()
+
+            else:
+                flux_copy(h).start()
+        for h in order:
+            for copy in sent[h]:
+                copy.start()
+    weight_load.wait()
+    owner = lax.broadcasted_iota(jnp.int32, (blocks, fluxes, block), 0)
+    blank = jnp.zeros((fluxes, block), jnp.int32)
+    early_spans = [d for d in range(spans) if d >= radius]
+    for group in (early_spans, [d for d in range(spans) if d < radius]):
+        for d in group:
+            if d != radius:
+                flux_copy(steps.index(d - radius)).wait_recv()
+        lefts = []
+        for d in group:
+            for c in range(slots):
+                used = (blank + remap_counts[0, d]) > c
+                piece = jnp.where(used, arrived[d, c].astype(jnp.float32), 0.0)
+                placed = jnp.where(owner == remap_target[d, 0, c], piece[None], 0.0)
+                lefts.append(placed.reshape(blocks * fluxes, block).astype(jnp.bfloat16))
+        term = product(
+            jnp.concatenate(lefts, axis=1),
+            weights[group[0] : group[-1] + 1].reshape(len(group) * slots * block, block),
+        )
+        if group is early_spans:
+            total[...] = term
+        else:
+            total[...] += term
+    pad = surface.shape[0] - tracers
+    for b in range(blocks):
+        run = slice(b * block, (b + 1) * block)
+        flux = total[b * fluxes : (b + 1) * fluxes, :] * wet[0:1, run].astype(jnp.float32)
+        flux_out[:, run] = flux
+        rows = []
+        for t in range(tracers):
+            value = coupling[t, 0] * flux[0:1, :]
+            for f in range(1, fluxes):
+                value = value + coupling[t, f] * flux[f : f + 1, :]
+            rows.append(value)
+        stacked = jnp.concatenate(rows + [jnp.zeros((pad, block), jnp.float32)], axis=0)
+        surface[:, run] = stacked
+        surface_rows[run, :] = jnp.transpose(stacked)
+    for h in order:
+        for row in range(picks):
+            cell = picks_smem[h, row // lanes, row % lanes]
+            surface_gathered[row] = surface_rows[cell]
+        surface_out[h] = jnp.transpose(surface_gathered[...])[:tracers]
+        side_copy(h, 2).start()
+    for h, t in held_back:
+        row_copy(h, t).start()
     ghosts = []
     line = jnp.zeros((1, lanes), jnp.int32)
     for h in range(hosts):
@@ -278,46 +367,6 @@
                 here == marks[i], pull, jnp.bfloat16(0)
             )
         keep[:, run] = 1.0 - product(ones, scatter[:, run])[0:1]
-    weight_load.wait()
-    owner = lax.broadcasted_iota(jnp.int32, (blocks, fluxes, block), 0)
-    blank = jnp.zeros((fluxes, block), jnp.int32)
-    for h in range(hosts):
-        flux_copy(h).wait_recv()
-    for d in range(spans):
-        pieces = []
-        for c in range(slots):
-            used = (blank + remap_counts[0, d]) > c
-            piece = jnp.where(used, arrived[d, c].astype(jnp.float32), 0.0)
-            placed = jnp.where(owner == remap_target[d, 0, c], piece[None], 0.0)
-            pieces.append(placed.reshape(blocks * fluxes, block).astype(jnp.bfloat16))
-        left = jnp.concatenate(pieces, axis=1)
-        term = product(left, weights[d].reshape(slots * block, block))
-        if d == 0:
-            total[...] = term
-        else:
-            total[...] += term
-    pad = surface.shape[0] - tracers
-    for b in range(blocks):
-        run = slice(b * block, (b + 1) * block)
-        flux = total[b * fluxes : (b + 1) * fluxes, :] * wet[0:1, run].astype(jnp.float32)
-        flux_out[:, run] = flux
-        rows = []
-        for t in range(tracers):
-            value = coupling[t, 0] * flux[0:1, :]
-            for f in range(1, fluxes):
-                value = value + coupling[t, f] * flux[f : f + 1, :]
-            rows.append(value)
-        stacked = jnp.concatenate(rows + [jnp.zeros((pad, block), jnp.float32)], axis=0)
-        surface[:, run] = stacked
-        surface_rows[run, :] = jnp.transpose(stacked)
-    for h in order:
-        for row in range(picks):
-            cell = picks_smem[h, row // lanes, row % lanes]
-            surface_gathered[row] = surface_rows[cell]
-        surface_out[h] = jnp.transpose(surface_gathered[...])[:tracers]
-        side_copy(h, 2).start()
-    for h, t in held_back:
-        row_copy(h, t).start()
     for k in range(blocks):
         run = slice(k * block, (k + 1) * block)
         first = jnp.broadcast_to(inverse[k, :, 0:1], (levels, block))
@@ -329,26 +378,58 @@
     ids = lax.broadcasted_iota(jnp.int32, (blocks, picks), 0)
     shift = block.bit_length() - 1
 
-    def correct(h):
-        for kind in range(3):
-            side_copy(h, kind).wait_recv()
+    half = hosts // 2
+    first_half = jnp.where(low, 0, half)
+
+    def correct(start, target):
+        for i in range(half):
+            h = start + i
+            for kind, (source, landing) in enumerate(
+                ((tips, tips_in), (halo_send.at[0], cells_in), (surface_out.at[0], surface_in))
+            ):
+                pltpu.make_async_remote_copy(
+                    src_ref=source,
+                    dst_ref=landing.at[h],
+                    send_sem=side_send_sem.at[kind, h],
+                    recv_sem=side_recv_sem.at[kind, h],
+                    device_id=(peer(1),),
+                    device_id_type=MESH,
+                ).wait_recv()
+            for t in range(tracers):
+                level = pl.ds(t * levels, levels)
+                pltpu.make_async_remote_copy(
+                    src_ref=picked.at[0, level],
+                    dst_ref=received.at[h, level],
+                    send_sem=halo_send_sem.at[h, t],
+                    recv_sem=halo_recv_sem.at[h, t],
+                    device_id=(peer(1),),
+                    device_id_type=MESH,
+                ).wait_recv()
+        for i in range(half):
+            h = start + i
+            numbers = cells_in[h]
+            where = jnp.concatenate([numbers[r : r + 1, :] for r in range(depth)], axis=1)
+            hit = ids == lax.shift_right_logical(where, shift)
+            tip = lax.dot_general(
+                tips_in[h],
+                jnp.where(hit, 1.0, 0.0).astype(jnp.bfloat16),
+                (((0,), (0,)), ((), ())),
+                preferred_element_type=jnp.float32,
+            )
+            tendency = surface_in[h]
+            for t in range(tracers):
+                level = slice(t * levels, (t + 1) * levels)
+                value = received[h, level, :].astype(jnp.float32) + tip * tendency[t : t + 1, :]
+                target[level, i * picks : (i + 1) * picks] = value.astype(jnp.bfloat16)
+
+    correct(first_half, early_values)
+    area = pl.ds(pl.multiple_of(first_half * picks, half * picks), half * picks)
+    for index in range(cells // rows):
+        run = slice(index * rows, (index + 1) * rows)
+        summed = product(early_values[...], scatter[area, run])
         for t in range(tracers):
-            row_copy(h, t).wait_recv()
-        where = jnp.concatenate([cells_in[h, r : r + 1, :] for r in range(depth)], axis=1)
-        hit = ids == lax.shift_right_logical(where, shift)
-        first = lax.dot_general(
-            tips_in[h],
-            jnp.where(hit, 1.0, 0.0).astype(jnp.bfloat16),
-            (((0,), (0,)), ((), ())),
-            preferred_element_type=jnp.float32,
-        )
-        for t in range(tracers):
-            level = slice(t * levels, (t + 1) * levels)
-            value = received[h, level, :].astype(jnp.float32) + first * surface_in[h, t : t + 1, :]
-            values[level, h * picks : (h + 1) * picks] = value.astype(jnp.bfloat16)
-
-    for h in order:
-        correct(h)
+            mixed[t, :, run] += summed[t * levels : (t + 1) * levels]
+    correct(half - first_half, values)
     for h in range(hosts):
         flux_copy(h).wait_send()
         for t in range(tracers):
@@ -357,20 +438,23 @@
             side_copy(h, kind).wait_send()
 
 
-def halo_kernel(values, scatter, kept, flux_in, flux_out, out, stage, sems):
+def halo_kernel(radius, values, scatter, kept, flux_in, flux_out, out, stage, sems):
     tracers, levels, cells = out.shape
+    count = values.shape[1]
+    start = jnp.where(lax.axis_index("patch") < radius, count, 0)
+    area = pl.ds(pl.multiple_of(start, count), count)
     flux_copy = pltpu.make_async_copy(flux_in, flux_out, sems.at[0])
     flux_copy.start()
     tile = min(TILE, cells)
     copies = [flux_copy]
     for index in range(cells // tile):
         run = slice(index * tile, (index + 1) * tile)
-        summed = product(values[...], scatter[:, run])
+        summed = product(values[...], scatter[area, run])
         for t in range(tracers):
             stage[t, :, run] = kept[t, :, run] + summed[t * levels : (t + 1) * levels]
-        area = pl.ds(index * tile, tile)
+        place = pl.ds(index * tile, tile)
         copy = pltpu.make_async_copy(
-            stage.at[:, :, area], out.at[:, :, area], sems.at[1 + index]
+            stage.at[:, :, place], out.at[:, :, place], sems.at[1 + index]
         )
         copy.start()
         copies.append(copy)
@@ -409,7 +493,7 @@
         out_shape=(
             pltpu.VMEM((fluxes, cells), jnp.float32),
             pltpu.VMEM((tracers, levels, cells), jnp.float32),
-            pltpu.VMEM((features, hosts * picks), jnp.bfloat16),
+            pltpu.VMEM((features, hosts // 2 * picks), jnp.bfloat16),
             pltpu.VMEM((hosts * picks, cells), jnp.bfloat16),
         ),
         in_specs=[hbm] * 12,
@@ -431,6 +515,7 @@
             pltpu.VMEM((blocks, levels, levels), jnp.float32),
             pltpu.VMEM((tracers, cells, levels), jnp.float32),
             pltpu.VMEM((picks, levels), jnp.float32),
+            pltpu.VMEM((features, hosts // 2 * picks), jnp.bfloat16),
             pltpu.VMEM((blocks, levels, 3 * levels), jnp.bfloat16),
             pltpu.VMEM((1, cells), jnp.float32),
             pltpu.VMEM((lead, cells), jnp.float32),
@@ -455,6 +540,7 @@
             dma((hosts, tracers)),
             dma((3, hosts)),
             dma((3, hosts)),
+            pltpu.SemaphoreType.REGULAR((hosts,)),
         ],
         compiler_params=pltpu.CompilerParams(
             collective_id=0, has_side_effects=True, vmem_limit_bytes=48 * 1024 * 1024
@@ -476,7 +562,7 @@
     )
     tile = min(TILE, cells)
     return pl.pallas_call(
-        halo_kernel,
+        functools.partial(halo_kernel, spans // 2),
         out_shape=(
             jax.ShapeDtypeStruct((fluxes, cells), jnp.float32),
             jax.ShapeDtypeStruct((tracers, levels, cells), jnp.float32),

time: 24.4 us -> 22 us (0.902)
  Pallas kernels: 23.6 us -> 21.2 us
    pallas_call x1, Pallas kernels: 20.4 us -> 18.8 us  [body(): pl.pallas_call(couple_kernel, out_shape=(pltpu.VMEM((fluxes, cells), jnp....]
    pallas_call x1, Pallas kernels: 3.21 us -> 2.39 us  [body(): pl.pallas_call(functools.partial(halo_kernel, spans // 2), out_shape=(jax...]
where the time goes in v3:
time: 22 us; the launch traced here: 21.8 us
  Pallas kernels  21.2 us (96%)
  between operations  0.64 us (3%)
    pallas_call x1, Pallas kernels, body(): pl.pallas_call(couple_kernel, out_shape=(pltpu.VMEM((fluxes, cells), jnp....  18.8 us
    pallas_call x1, Pallas kernels, body(): pl.pallas_call(functools.partial(halo_kernel, spans // 2), out_shape=(jax...  2.39 us

profile of v3, /device:TPU:0, one launch (start us, length us, event | category | flops | bytes accessed | tf_op | source)
XLA Modules:
  0.0 21.8 jit_solution(9303357477882436188)
XLA Ops:
  0.6 18.8 %couple.1 = (f32[8,4096]{1,0:T(8,128)S(1)}, f32[2,128,4096]{2,1,0:T(8,128)S(1)}, bf16[256,512]{1,0:T(8,128)(2,1)S(1)}, bf16[1024,4096]{1,0:T(8,128)(2,1)S(1)}) custom-call(s32[5,1,8]{2,1,0:T(1,128)} %bitcast.4, s32[5,1,8]{2,1,0:T(1,128)} %bitcast.5, s32[1,5]{1,0:T(1,128)} %counts_hbm.1, f32[2,8]{1,0:T(2,128)} %coupling_hbm.1, s32[1,4]{1,0:T(1,128)} %halo_rows_hbm.1, ...), custom_call_target="tpu_custom_call" | custom-call | tf_op jit(solution)/shard_map/couple/pallas_call | solution.py:491
  19.4 2.4 %halo.1 = (f32[8,4096]{1,0:T(8,128)}, f32[2,128,4096]{2,1,0:T(8,128)}) custom-call(bf16[256,512]{1,0:T(8,128)(2,1)S(1)} %get-tuple-element.6.values, bf16[1024,4096]{1,0:T(8,128)(2,1)S(1)} %get-tuple-element.7.scatter, f32[2,128,4096]{2,1,0:T(8,128)S(1)} %get-tuple-element.8.kept, f32[8,4096]{1,0:T(8,128)S(1)} %get-tuple-element.9.flux_in), custom_call_target="tpu_custom_call" | custom-call | tf_op jit(solution)/shard_map/halo/pallas_call | solution.py:564
